TPU v7x, 32 devices: a whole 2x2x4 slice. The times are simulated.
32 devices in a mesh: orient: 4 (over z), slab: 8 (over y, x, core).
Axes of the slice: x: 2, y: 2, z: 4, core: 2. Of those that a mesh axis runs over, the one named last changes fastest.
Arguments:
- polarization: bfloat16 [8, 2, 3, 8, 9216], P('orient', None, None, 'slab'), may hold values from -6 to 6
- occupied: int32 [8, 9216], P('slab'), may hold values from 0 to 1, as said below
- orient_table: int32 [8, 2], replicated, may hold values from 0 to 15
- dir_index: int32 [2048, 2], replicated, may hold values from 0 to 179
Outputs:
- mueller: float32 [4, 2048], P(None, 'slab')
Inputs may be any that keep to these rules, and one draw needn't show every extreme that they name: 1 marks an occupied dipole cell.
All inputs are finite; a program needn't handle non-finite values.
Results may differ from a plain program's by a relative error of at most 0.00087.
Values may be sent and summed in bfloat16 or wider, within the bound.
A program may use at most 64 MiB of HBM per device.

v0:
```python
import functools
import math

import jax
import jax.numpy as jnp
from jax import lax
from jax.experimental import pallas as pl
from jax.experimental.pallas import tpu as pltpu
from jax.sharding import PartitionSpec as P

GX = 96
ORIENT_GRID = 16
THETA_GRID = 180
YL = 4
MB = 4
wave_step = 0.4
MESH = pl.DeviceIdType.MESH
F32 = jnp.float32
BF16 = jnp.bfloat16


def sincos(angle):
    quarter = jnp.round(angle * (2.0 / math.pi))
    rest = angle - quarter * 1.5703125
    rest = rest - quarter * 4.83826794896619e-4
    square = rest * rest
    sine = rest + rest * square * (
        -1.6666654611e-1 + square * (8.3321608736e-3 + square * -1.9515295891e-4)
    )
    cosine = 1.0 - 0.5 * square + square * square * (
        4.166664568298827e-2
        + square * (-1.388731625493765e-3 + square * 2.443315711809948e-5)
    )
    turns = quarter.astype(jnp.int32)
    odd = (turns & 1) == 1
    sin_sign = jnp.where((turns & 2) == 2, -1.0, 1.0)
    cos_sign = jnp.where(((turns + 1) & 2) == 2, -1.0, 1.0)
    return (
        jnp.where(odd, cosine, sine) * sin_sign,
        jnp.where(odd, sine, cosine) * cos_sign,
    )


def flip_index(me, step, size):
    if size & (size - 1):
        return (me + step) % size
    result, bit = 0, 1
    while bit < size:
        result = result + ((me // bit) % 2 + (step // bit) % 2) % 2 * bit
        bit *= 2
    return result


def kernel(
    slab_size, orient_size, cells_all,
    table_hbm, dirs_hbm, pol_ref, occ_ref, out_ref,
    table_ref, dirs_ref, normal, trig, basis, held_pol, held_occ, mask, phases, sent, landed, parts,
    load_sem, send_sem, recv_sem, part_send, part_recv,
):
    slab = lax.axis_index("slab")
    orient = lax.axis_index("orient")
    loads = [
        pltpu.make_async_copy(dirs_hbm, dirs_ref, load_sem.at[2]),
        pltpu.make_async_copy(table_hbm, table_ref, load_sem.at[3]),
        pltpu.make_async_copy(pol_ref, held_pol, load_sem.at[0]),
        pltpu.make_async_copy(occ_ref, held_occ, load_sem.at[1]),
    ]
    for load in loads:
        load.start()
    local_orients, components, planes, _, cells = pol_ref.shape
    all_orients = table_ref.shape[1]
    width = dirs_ref.shape[2]
    group = sent.shape[1] // 2
    span = 2 * group
    depth = YL * GX
    pairs = cells // depth // 2

    barrier = pltpu.get_barrier_semaphore()
    for step in range(1, slab_size):
        pl.semaphore_signal(
            barrier, inc=1, device_id=(orient, flip_index(slab, step, slab_size)),
            device_id_type=MESH,
        )
    for step in range(1, orient_size):
        pl.semaphore_signal(
            barrier, inc=1, device_id=((orient + step) % orient_size, slab),
            device_id_type=MESH,
        )

    loads[0].wait()
    dirs = dirs_ref[...].astype(F32)
    azimuth = dirs[:, 1, :] * (2.0 * math.pi / THETA_GRID)
    sin_p, cos_p = sincos((dirs[:, 0, :] + 0.5) * (math.pi / THETA_GRID))
    sin_a, cos_a = sincos(azimuth)
    normal[0] = sin_p * cos_a
    normal[1] = sin_p * sin_a
    normal[2] = cos_p
    normal[3] = sin_p
    normal[4] = azimuth

    line = lax.broadcasted_iota(jnp.int32, (24, 1), 0)
    middle = 0.5 * (YL - 1)
    coef_x = jnp.where(
        line < 8, line.astype(F32), jnp.where(line == 16, 8.0, 0.0)
    ) * wave_step
    coef_y = jnp.where(
        (line >= 8) & (line < 16), line.astype(F32) - 7.5,
        jnp.where(
            line == 17, 2.0 * YL,
            jnp.where(line == 18, middle, jnp.where(line == 19, YL + middle, 0.0)),
        ),
    ) * wave_step

    together = math.gcd(slab_size, 4)

    def make_tables(block, carry):
        for inner in range(together):
            index = block * together + inner
            row = pl.ds(index, 1)
            for plane in range(planes):
                depth_at = (slab * planes + plane).astype(F32)
                coef_z = jnp.where((line == 18) | (line == 19), depth_at, 0.0) * wave_step
                angle = (
                    coef_x * normal[0, row, :] + coef_y * normal[1, row, :]
                    + coef_z * normal[2, row, :]
                )
                sine, cosine = sincos(angle)
                trig[0, plane, index] = cosine
                trig[1, plane, index] = sine
        return carry

    lax.fori_loop(0, slab_size // together, make_tables, 0)

    loads[1].wait()
    tilt_row = lax.broadcasted_iota(jnp.int32, (all_orients, width), 0)
    tilts = jnp.zeros((all_orients, width), F32)
    for o in range(all_orients):
        tilts = jnp.where(tilt_row == o, table_ref[1, o].astype(F32), tilts)
    weights = sincos((tilts + 0.5) * (math.pi / ORIENT_GRID))[0]
    share = 1.0 / (jnp.sum(weights, axis=0, keepdims=True) * cells_all)
    own = pl.ds(slab, 1)
    for o in range(local_orients):
        turn = table_ref[0, orient * local_orients + o].astype(F32)
        tilt = table_ref[1, orient * local_orients + o].astype(F32)
        turns = jnp.full((1, width), turn, F32) * (2.0 * math.pi / ORIENT_GRID)
        sin_q, cos_q = sincos(normal[4, own, :] - turns)
        scaled = (jnp.full((1, width), tilt, F32) + 0.5) * (math.pi / ORIENT_GRID)
        basis[o, 0:1] = sin_q
        basis[o, 1:2] = cos_q
        basis[o, 2:3] = sincos(scaled)[0] * share

    for load in loads[2:]:
        load.wait()

    def place(block, carry):
        for plane in range(planes):
            for part in range(MB):
                at = pl.ds(pl.multiple_of((block * MB + part) * depth, 128), depth)
                kept = held_occ[pl.ds(plane, 1), at].astype(F32).astype(BF16)
                pieces = [
                    held_pol[o, c, plane, :, at]
                    for o in range(local_orients)
                    for c in range(components)
                ]
                rows = jnp.concatenate(pieces, axis=0) * kept
                mask[plane, block, part * group : (part + 1) * group, :] = rows
        return carry

    lax.fori_loop(0, cells // depth // MB, place, 0)

    def generate(index, plane, slot):
        cos_t = trig[0, plane, index]
        sin_t = trig[1, plane, index]
        step_c, step_s = cos_t[16:17], sin_t[16:17]
        tile_c, tile_s = cos_t[0:8], sin_t[0:8]

        def put(kind, first, values):
            high = values.astype(BF16)
            phases[slot, kind, first : first + 16] = high
            phases[slot, kind, depth + first : depth + first + 16] = (
                values - high.astype(F32)
            ).astype(BF16)

        for turn in range(GX // 16):
            next_c = tile_c * step_c - tile_s * step_s
            next_s = tile_s * step_c + tile_c * step_s
            line_c = jnp.concatenate([tile_c, next_c], axis=0)
            line_s = jnp.concatenate([tile_s, next_s], axis=0)
            for y in range(YL // 2):
                y_c, y_s = cos_t[8 + y : 9 + y], sin_t[8 + y : 9 + y]
                cc, ss = line_c * y_c, line_s * y_s
                sc, cs = line_s * y_c, line_c * y_s
                above = (YL // 2 + y) * GX + turn * 16
                below = (YL // 2 - 1 - y) * GX + turn * 16
                put(0, above, cc - ss)
                put(0, below, cc + ss)
                put(1, above, sc + cs)
                put(1, below, sc - cs)
            if turn + 1 < GX // 16:
                tile_c = next_c * step_c - next_s * step_s
                tile_s = next_s * step_c + next_c * step_s

    def multiply(index, plane, slot):
        masked = mask[plane].reshape(pairs * span, depth)
        masked = jnp.concatenate([masked, masked], axis=1)
        real = jnp.dot(masked, phases[slot, 0], preferred_element_type=F32)
        imag = jnp.dot(masked, phases[slot, 1], preferred_element_type=F32)
        cos_t = trig[0, plane, index]
        sin_t = trig[1, plane, index]
        jump_c, jump_s = cos_t[17:18], sin_t[17:18]
        acc_c, acc_s = real[(pairs - 1) * span :], imag[(pairs - 1) * span :]
        for pair in range(pairs - 2, -1, -1):
            part = slice(pair * span, (pair + 1) * span)
            acc_c, acc_s = (
                acc_c * jump_c - acc_s * jump_s + real[part],
                acc_s * jump_c + acc_c * jump_s + imag[part],
            )
        lower = lax.broadcasted_iota(jnp.int32, (span, width), 0) < group
        last_c = jnp.where(lower, cos_t[18:19], cos_t[19:20])
        last_s = jnp.where(lower, sin_t[18:19], sin_t[19:20])
        whole_c = acc_c * last_c - acc_s * last_s
        whole_s = acc_s * last_c + acc_c * last_s
        whole_c = whole_c + jnp.concatenate([whole_c[group:], whole_c[:group]], axis=0)
        whole_s = whole_s + jnp.concatenate([whole_s[group:], whole_s[:group]], axis=0)
        return jnp.where(lower, whole_c, whole_s)

    def slab_copy(step):
        peer = flip_index(slab, step, slab_size)
        return pltpu.make_async_remote_copy(
            src_ref=sent.at[step],
            dst_ref=landed.at[step],
            send_sem=send_sem.at[step],
            recv_sem=recv_sem.at[step],
            device_id=(orient, peer),
            device_id_type=MESH,
        )

    def target(count):
        return flip_index(slab, slab_size - 1 - count, slab_size)

    def stage(count, slot, last):
        index = target(count)
        step = slab_size - 1 - count
        total = None
        for plane in range(planes):
            now = (slot + plane) % 2
            if plane + 1 < planes:
                generate(index, plane + 1, 1 - now)
            elif not last:
                generate(target(count + 1), 0, 1 - now)
            here = multiply(index, plane, now)
            total = here if total is None else total + here
        sent[step] = total
        if not last:
            slab_copy(step).start()

    def advance(turn, carry):
        stage(2 * turn, 0, False)
        stage(2 * turn + 1, planes % 2, False)
        return carry

    generate(target(0), 0, 0)
    pl.semaphore_wait(barrier, slab_size - 1 + orient_size - 1)
    lax.fori_loop(0, slab_size // 2 - 1, advance, 0)
    stage(slab_size - 2, 0, False)
    stage(slab_size - 1, planes % 2, True)

    amplitude = sent[0]
    for step in range(slab_size - 1, 0, -1):
        slab_copy(step).wait_recv()
        amplitude = amplitude + landed[step]

    sin_p, cos_p = normal[3, own, :], normal[2, own, :]
    results = [0.0, 0.0, 0.0, 0.0]
    for o in range(local_orients):
        sin_q, cos_q, weight = basis[o, 0:1], basis[o, 1:2], basis[o, 2:3]

        def entry(p, c, r):
            at = r * group + (o * 3 + c) * 2 + p
            return amplitude[at : at + 1]

        def project(p, r):
            first, second, third = entry(p, 0, r), entry(p, 1, r), entry(p, 2, r)
            par = cos_p * (first * cos_q + second * sin_q) - sin_p * third
            across = second * cos_q - first * sin_q
            return par, across

        ul_r, ur_r = project(0, 0)
        ul_i, ur_i = project(0, 1)
        ll_r, lr_r = project(1, 0)
        ll_i, lr_i = project(1, 1)
        lr2 = lr_r * lr_r + lr_i * lr_i
        ul2 = ul_r * ul_r + ul_i * ul_i
        ur2 = ur_r * ur_r + ur_i * ur_i
        ll2 = ll_r * ll_r + ll_i * ll_i
        found = (
            0.5 * (lr2 + ul2 + ur2 + ll2),
            0.5 * (ul2 - lr2 + ll2 - ur2),
            lr_r * ul_r + lr_i * ul_i + ur_r * ll_r + ur_i * ll_i,
            ul_r * lr_i - ul_i * lr_r + ll_r * ur_i - ll_i * ur_r,
        )
        results = [old + weight * new for old, new in zip(results, found)]

    parts[orient] = jnp.concatenate(results, axis=0)

    def part_copy(step):
        return pltpu.make_async_remote_copy(
            src_ref=parts.at[orient],
            dst_ref=parts.at[orient],
            send_sem=part_send.at[step],
            recv_sem=part_recv.at[step],
            device_id=((orient + step) % orient_size, slab),
            device_id_type=MESH,
        )

    for step in range(1, orient_size):
        part_copy(step).start()
    for step in range(slab_size - 1, 0, -1):
        slab_copy(step).wait_send()
    for step in range(1, orient_size):
        back = (orient + orient_size - step) % orient_size
        pltpu.make_async_remote_copy(
            src_ref=parts.at[orient],
            dst_ref=parts.at[back],
            send_sem=part_send.at[step],
            recv_sem=part_recv.at[step],
            device_id=(back, slab),
            device_id_type=MESH,
        ).wait_recv()
    summed = parts[0]
    for o in range(1, orient_size):
        summed = summed + parts[o]
    out_ref[...] = summed
    for step in range(1, orient_size):
        part_copy(step).wait_send()


def shards(slab_size, orient_size, polarization, occupied, orient_table, dir_index):
    orients, _, components, planes, cells = polarization.shape
    group = orients * 6
    depth = YL * GX
    pol = polarization.transpose(0, 2, 3, 1, 4)
    width = dir_index.shape[0] // slab_size
    dirs = dir_index.T.reshape(2, slab_size, width).transpose(1, 0, 2)
    vmem = pl.BlockSpec(memory_space=pltpu.VMEM)
    anywhere = pl.BlockSpec(memory_space=pltpu.HBM)
    return pl.pallas_call(
        functools.partial(
            kernel, slab_size, orient_size, float(planes * slab_size * cells)
        ),
        out_shape=pltpu.VMEM((4, width), F32),
        in_specs=[anywhere] * 4,
        out_specs=vmem,
        scratch_shapes=[
            pltpu.SMEM((2, orient_table.shape[0]), jnp.int32),
            pltpu.VMEM(dirs.shape, jnp.int32),
            pltpu.VMEM((5, slab_size, width), F32),
            pltpu.VMEM((2, planes, slab_size, 24, width), F32),
            pltpu.VMEM((orients, 3, width), F32),
            pltpu.VMEM(pol.shape, BF16),
            pltpu.VMEM(occupied.shape, jnp.int32),
            pltpu.VMEM((planes, cells // depth // MB, MB * group, depth), BF16),
            pltpu.VMEM((2, 2, 2 * depth, width), BF16),
            pltpu.VMEM((slab_size, 2 * group, width), F32),
            pltpu.VMEM((slab_size, 2 * group, width), F32),
            pltpu.VMEM((orient_size, 4, width), F32),
            pltpu.SemaphoreType.DMA((4,)),
            pltpu.SemaphoreType.DMA((slab_size,)),
            pltpu.SemaphoreType.DMA((slab_size,)),
            pltpu.SemaphoreType.DMA((orient_size,)),
            pltpu.SemaphoreType.DMA((orient_size,)),
        ],
        compiler_params=pltpu.CompilerParams(
            collective_id=0, has_side_effects=True
        ),
    )(orient_table.T, dirs, pol, occupied)


def solution(mesh):
    return jax.shard_map(
        functools.partial(shards, mesh.shape["slab"], mesh.shape["orient"]),
        mesh=mesh,
        in_specs=(P("orient", None, None, "slab", None), P("slab", None), P(), P()),
        out_specs=P(None, "slab"),
        check_vma=False,
    )
```

profile of v0, /device:TPU:0, one launch (start us, length us, event | category | flops | bytes accessed | tf_op | source)
XLA Modules:
  0.0 15.9 jit_solution(11049052317267886995)
XLA Ops:
  0.0 15.3 %shard_map.46 = f32[4,256]{1,0:T(4,128)S(1)} custom-call(s32[2,8]{1,0:T(2,128)} %bitcast.9, s32[8,2,256]{2,1,0:T(2,128)} %bitcast.8, bf16[2,3,1,2,9216]{4,3,2,1,0:T(2,128)(2,1)} %bitcast.7, s32[1,9216]{1,0:T(1,128)} %occ_ref.1), custom_call_target="tpu_custom_call" | custom-call | tf_op jit(solution)/shard_map/pallas_call | solution.py:347
  15.3 0.6 %copy.6 = f32[4,256]{1,0:T(4,128)} copy(f32[4,256]{1,0:T(4,128)S(1)} %shard_map.46) | data formatting | bytes 8192
where the time goes:
time: 16.1 us; the launch traced here: 15.9 us
  Pallas kernels  15.3 us (95%)
  local copies, waits for them, and re-layouts  0.6 us (4%)
    pallas_call x1, Pallas kernels, shards(): pl.pallas_call(functools.partial(kernel, slab_size, orient_size, float(pl...  15.3 us
    unnamed x1, local copies, waits for them, and re-layouts  0.6 us

commit v1 on v0

v1 whole, which is shorter than its diff:
```python
import functools
import math

import jax
import jax.numpy as jnp
import numpy as np
from jax import lax
from jax.experimental import pallas as pl
from jax.experimental.pallas import tpu as pltpu
from jax.sharding import PartitionSpec as P

GX = 96
ORIENT_GRID = 16
THETA_GRID = 180
LANES = 128
RX = 32
RY = 24
wave_step = 0.4
MESH = pl.DeviceIdType.MESH
F32 = jnp.float32
BF16 = jnp.bfloat16
PER = LANES // math.gcd(LANES, GX)
TILES = GX // math.gcd(LANES, GX)
HALF = RX // 2
GROUPS = RY // 2 * RX // LANES


def sincos(angle):
    quarter = jnp.round(angle * (2.0 / math.pi))
    rest = angle - quarter * 1.5703125
    rest = rest - quarter * 4.83826794896619e-4
    square = rest * rest
    sine = rest + rest * square * (
        -1.6666654611e-1 + square * (8.3321608736e-3 + square * -1.9515295891e-4)
    )
    cosine = 1.0 - 0.5 * square + square * square * (
        4.166664568298827e-2
        + square * (-1.388731625493765e-3 + square * 2.443315711809948e-5)
    )
    turns = quarter.astype(jnp.int32)
    odd = (turns & 1) == 1
    sin_sign = jnp.where((turns & 2) == 2, -1.0, 1.0)
    cos_sign = jnp.where(((turns + 1) & 2) == 2, -1.0, 1.0)
    return (
        jnp.where(odd, cosine, sine) * sin_sign,
        jnp.where(odd, sine, cosine) * cos_sign,
    )


def prolate(length, count):
    band = math.cos(wave_step)
    at = np.arange(length)
    near = at[1:] * (length - at[1:]) / 2.0
    matrix = np.diag(((length - 1 - 2 * at) / 2.0) ** 2 * band) + np.diag(near, 1) + np.diag(near, -1)
    vectors = np.linalg.eigh(matrix)[1][:, ::-1][:, :count]
    middle = at - (length - 1) / 2.0
    even, odd = vectors[:, 0::2], vectors[:, 1::2]
    even = (even + even[::-1]) / 2.0
    odd = (odd - odd[::-1]) / 2.0
    even = even * np.where(even[length // 2] < 0, -1.0, 1.0)
    odd = odd * np.where(odd[length // 2] < 0, -1.0, 1.0)
    return even, odd


def split(values):
    high = np.asarray(values, np.float32).astype(jnp.bfloat16)
    low = (np.asarray(values, np.float64) - high.astype(np.float64)).astype(np.float32)
    return high, low.astype(jnp.bfloat16)


def tables(cells):
    lines = cells // GX
    tiles = cells // LANES
    even_x, odd_x = prolate(GX, RX)
    even_y, odd_y = prolate(lines, RY)
    both_y = np.stack([even_y, odd_y], axis=2).reshape(lines, RY)
    first = np.zeros((2, TILES, 2, RY, tiles, 2))
    for tile in range(tiles):
        line = tile * LANES // GX
        for next_line in range(2):
            for p in range(2):
                first[p, tile % TILES, next_line, :, tile, p] = both_y[line + next_line]
    first = first.reshape(2 * TILES * 2 * RY, tiles * 2)
    rows = np.concatenate(split(first), axis=1)
    block = np.concatenate([even_x, odd_x], axis=1)
    columns = np.concatenate(split(np.tile(block, (1, LANES // RX))), axis=0)
    pieces = []
    for even, odd in ((even_x, odd_x), (even_y, odd_y)):
        for part in (even, odd):
            length = part.shape[0]
            half = np.zeros((HALF, length // 2))
            half[: part.shape[1]] = 2.0 * part[length // 2 :].T
            pieces.append(half)
    trig = np.stack(pieces)
    high, low = split(trig)
    trig = np.concatenate([high, high, low], axis=2)
    return rows, columns, trig.reshape(4 * HALF, -1)


def high_low(values):
    high = values.astype(BF16)
    return high, (values - high.astype(F32)).astype(BF16)


def kernel(
    slab_size, orient_size, planes, cells_all,
    pol_hbm, occ_hbm, table_hbm, dirs_hbm, rows_hbm, columns_hbm, trig_hbm, out_ref,
    held_pol, held_occ, table_ref, dirs_ref, rows_ref, columns_ref, trig_ref,
    twice, coef, found, turned, vv, landed, mine, parts,
    load_sem, send_sem, recv_sem, part_send, part_recv,
):
    slab = lax.axis_index("slab")
    orient = lax.axis_index("orient")
    partner = slab + 1 - 2 * (slab % 2)
    width = dirs_ref.shape[1]
    all_orients = table_ref.shape[1]
    tiles = held_occ.shape[0] // planes
    pair_rows = 2 * tiles
    blocks = held_pol.shape[0] // (planes * pair_rows)
    orients = blocks // 3
    group = blocks * 2
    loads = [
        pltpu.make_async_copy(occ_hbm, held_occ, load_sem.at[0]),
        pltpu.make_async_copy(pol_hbm, held_pol, load_sem.at[1]),
        pltpu.make_async_copy(rows_hbm, rows_ref, load_sem.at[2]),
        pltpu.make_async_copy(columns_hbm, columns_ref, load_sem.at[3]),
        pltpu.make_async_copy(dirs_hbm.at[partner], dirs_ref, load_sem.at[4]),
        pltpu.make_async_copy(table_hbm, table_ref, load_sem.at[5]),
        pltpu.make_async_copy(trig_hbm, trig_ref, load_sem.at[6]),
    ]
    for load in loads:
        load.start()

    barrier = pltpu.get_barrier_semaphore()
    for step in range(1, slab_size):
        pl.semaphore_signal(
            barrier, inc=1, device_id=(orient, (slab + step) % slab_size),
            device_id_type=MESH,
        )
    for step in range(1, orient_size):
        pl.semaphore_signal(
            barrier, inc=1, device_id=((orient + step) % orient_size, partner),
            device_id_type=MESH,
        )

    for load in loads[:4]:
        load.wait()
    lane = lax.broadcasted_iota(jnp.int32, (1, LANES), 1)
    kept = held_occ[...].astype(F32)
    twice[pl.ds(0, planes * tiles, stride=2), :] = kept
    twice[pl.ds(1, planes * tiles, stride=2), :] = kept
    columns = [columns_ref[0:GX, :]] * PER, [columns_ref[GX : 2 * GX, :]] * PER
    columns = jnp.concatenate(columns[0] + columns[1] + columns[0], axis=0)
    step_blocks = 2 - blocks % 2
    for plane in range(planes):
        mask = twice[plane * pair_rows : (plane + 1) * pair_rows, :].astype(BF16)
        for start in range(0, blocks, step_blocks):
            masked = jnp.concatenate(
                [
                    held_pol[pl.ds(((start + i) * planes + plane) * pair_rows, pair_rows), :] * mask
                    for i in range(step_blocks)
                ],
                axis=1,
            )
            lines = jnp.dot(
                rows_ref[...], jnp.concatenate([masked, masked], axis=0),
                preferred_element_type=F32,
            )
            stacked = []
            for i in range(step_blocks):
                for p in range(2):
                    wide = []
                    for j in range(TILES):
                        base = (p * TILES + j) * 2 * RY
                        at = slice(i * LANES, (i + 1) * LANES)
                        limit = GX - j * LANES % GX
                        wide.append(
                            jnp.where(
                                lane < limit,
                                lines[base : base + RY, at],
                                lines[base + RY : base + 2 * RY, at],
                            )
                        )
                    stacked.append(jnp.concatenate(wide, axis=1))
            high, low = high_low(jnp.concatenate(stacked, axis=0))
            small = jnp.dot(
                jnp.concatenate([high, high, low], axis=1), columns,
                preferred_element_type=F32,
            )
            count = step_blocks * 2 * RY
            coef[start * 2 * RY : start * 2 * RY + count, :] = small
            coef[(blocks + start) * 2 * RY : (blocks + start) * 2 * RY + count, :] = small
        lines_of = [coef[pl.ds(ky, 2 * group, stride=RY), :] for ky in range(RY)]
        upper = lane % RX >= HALF
        is_low = lax.broadcasted_iota(jnp.int32, (2 * group, LANES), 0) >= group
        for imag in range(2):
            for g in range(GROUPS):
                whole = None
                for q in range(LANES // RX - 1, -1, -1):
                    a = g * (LANES // RX) + q
                    one, two = lines_of[2 * a + imag], lines_of[2 * a + 1 - imag]
                    block = jnp.where(upper, two, one)
                    whole = block if whole is None else jnp.where(lane < (q + 1) * RX, block, whole)
                high = whole.astype(BF16).astype(F32)
                at = (imag * GROUPS + g) * LANES
                landed[slab, plane, 0 : 2 * group, at : at + LANES] = jnp.where(
                    is_low, whole - high, high
                ).astype(BF16)

    pl.semaphore_wait(barrier, slab_size - 1 + orient_size - 1)
    order = [at + 1 - 2 * (at % 2) for at in range(slab_size)]

    def slab_copy(source, target):
        piece = landed.at[source, :, pl.ds(0, 2 * group), :]
        return pltpu.make_async_remote_copy(
            src_ref=piece,
            dst_ref=piece,
            send_sem=send_sem.at[target],
            recv_sem=recv_sem.at[source],
            device_id=(orient, target),
            device_id_type=MESH,
        )

    for target in order:
        @pl.when(slab != target)
        def _():
            slab_copy(slab, target).start()

    for load in loads[4:]:
        load.wait()
    dirs = dirs_ref[...].astype(F32)
    is_polar = lax.broadcasted_iota(jnp.int32, (2, width), 0) == 0
    angles = jnp.where(
        is_polar, (dirs + 0.5) * (math.pi / THETA_GRID), dirs * (2.0 * math.pi / THETA_GRID)
    )
    sines, cosines = sincos(angles)
    sin_p, cos_p = sines[0:1], cosines[0:1]
    sin_a, cos_a = sines[1:2], cosines[1:2]
    azimuth = angles[1:2]
    normals = (sin_p * cos_a, sin_p * sin_a)
    parts_of = []
    for axis in range(2):
        length = trig_ref.shape[1] // 3
        step = lax.broadcasted_iota(jnp.int32, (length, width), 0).astype(F32) + 0.5
        sine, cosine = sincos(step * (wave_step * normals[axis]))
        for kind, wave in enumerate((cosine, sine)):
            high, low = high_low(wave)
            at = (axis * 2 + kind) * HALF
            parts_of.append(
                jnp.dot(
                    trig_ref[at : at + HALF, :],
                    jnp.concatenate([high, low, high], axis=0),
                    preferred_element_type=F32,
                )
            )
    even_x, odd_x, even_y, odd_y = parts_of
    deep = RY // 2 * RX
    for a in range(RY // 2):
        one, two = even_y[a : a + 1], odd_y[a : a + 1]
        for kind, pieces in enumerate(
            (
                (even_x * one, -(odd_x * two)),
                (even_x * two, odd_x * one),
            )
        ):
            high, low = high_low(jnp.concatenate(pieces, axis=0))
            vv[kind, a * RX : (a + 1) * RX, :] = high
            vv[kind, deep + a * RX : deep + (a + 1) * RX, :] = low

    tilt_row = lax.broadcasted_iota(jnp.int32, (all_orients, width), 0)
    tilts = jnp.zeros((all_orients, width), F32)
    for o in range(all_orients):
        tilts = jnp.where(tilt_row == o, table_ref[1, o].astype(F32), tilts)
    weights = sincos((tilts + 0.5) * (math.pi / ORIENT_GRID))[0]
    share = 1.0 / (jnp.sum(weights, axis=0, keepdims=True) * cells_all)
    own_row = lax.broadcasted_iota(jnp.int32, (2 * orients, width), 0) % orients
    turns = jnp.zeros((2 * orients, width), F32)
    tilt = jnp.zeros((2 * orients, width), F32)
    for o in range(orients):
        turns = jnp.where(own_row == o, table_ref[0, orient * orients + o].astype(F32), turns)
        tilt = jnp.where(own_row == o, table_ref[1, orient * orients + o].astype(F32), tilt)
    sin_q, cos_q = sincos(azimuth - turns * (2.0 * math.pi / ORIENT_GRID))
    weight = sincos((tilt + 0.5) * (math.pi / ORIENT_GRID))[0] * share
    depth_at = lax.broadcasted_iota(jnp.int32, (slab_size * planes, width), 0).astype(F32)
    sin_z, cos_z = sincos(depth_at * (wave_step * cos_p))
    turned[0] = cos_z
    turned[1] = sin_z

    for source in order[::-1]:
        @pl.when(slab != source)
        def _():
            slab_copy(source, slab).wait_recv()

    space = landed.shape[2]
    everything = landed[...].reshape(slab_size * planes * space, 2 * deep)
    real_in, imag_in = everything[:, :deep], everything[:, deep:]
    real = jnp.dot(
        jnp.concatenate([real_in, real_in], axis=1), vv[0], preferred_element_type=F32
    )
    imag = jnp.dot(
        jnp.concatenate([imag_in, imag_in], axis=1), vv[1], preferred_element_type=F32
    )
    total_r = total_i = None
    for z in range(slab_size * planes):
        at = slice(z * space, z * space + 2 * group)
        c, s = turned[0, z : z + 1, :], turned[1, z : z + 1, :]
        now_r = real[at] * c - imag[at] * s
        now_i = imag[at] * c + real[at] * s
        total_r = now_r if total_r is None else total_r + now_r
        total_i = now_i if total_i is None else total_i + now_i
    total_r, total_i = total_r[:group] + total_r[group:], total_i[:group] + total_i[group:]
    piece = min(width, LANES)
    for h in range(width // piece):
        found[h, :group, :piece] = total_r[:, h * piece : (h + 1) * piece]
        found[h, group:, :piece] = total_i[:, h * piece : (h + 1) * piece]

    def entry(c, p):
        return jnp.concatenate(
            [
                found[h, pl.ds(2 * c + p, 2 * orients, stride=6), :][:, :piece]
                for h in range(width // piece)
            ],
            axis=1,
        )

    par, across = [], []
    for p in range(2):
        one, two, three = entry(0, p), entry(1, p), entry(2, p)
        par.append(cos_p * (one * cos_q + two * sin_q) - sin_p * three)
        across.append(two * cos_q - one * sin_q)
    par_square = par[0] * par[0] + par[1] * par[1]
    across_square = across[0] * across[0] + across[1] * across[1]

    def swap(values):
        return jnp.concatenate([values[orients:], -values[:orients]], axis=0)

    elements = (
        0.5 * (par_square + across_square),
        0.5 * (par_square - across_square),
        across[1] * par[0] + across[0] * par[1],
        par[0] * swap(across[1]) + par[1] * swap(across[0]),
    )
    mine[...] = jnp.concatenate(
        [jnp.sum(element * weight, axis=0, keepdims=True) for element in elements], axis=0
    )

    def part_copy(step):
        return pltpu.make_async_remote_copy(
            src_ref=mine,
            dst_ref=parts.at[orient],
            send_sem=part_send.at[step],
            recv_sem=part_recv.at[step],
            device_id=((orient + step) % orient_size, partner),
            device_id_type=MESH,
        )

    for step in range(orient_size):
        part_copy(step).start()
    for target in order:
        @pl.when(slab != target)
        def _():
            slab_copy(slab, target).wait_send()
    for step in range(orient_size):
        back = (orient + orient_size - step) % orient_size
        pltpu.make_async_remote_copy(
            src_ref=mine,
            dst_ref=parts.at[back],
            send_sem=part_send.at[step],
            recv_sem=part_recv.at[step],
            device_id=(back, partner),
            device_id_type=MESH,
        ).wait_recv()
    summed = parts[0]
    for o in range(1, orient_size):
        summed = summed + parts[o]
    out_ref[...] = summed
    for step in range(orient_size):
        part_copy(step).wait_send()


def shards(slab_size, orient_size, polarization, occupied, orient_table, dir_index):
    orients, _, components, planes, cells = polarization.shape
    group = orients * 6
    tiles = cells // LANES
    width = dir_index.shape[0] // slab_size
    pol = polarization.reshape(orients, 2, components, planes, tiles, LANES)
    pol = pol.transpose(0, 2, 3, 4, 1, 5).reshape(-1, LANES)
    occ = occupied.reshape(planes * tiles, LANES)
    dirs = dir_index.T.reshape(2, slab_size, width).transpose(1, 0, 2)
    rows, columns, trig = (jnp.asarray(table) for table in tables(cells))
    space = -(-2 * group // 16) * 16
    deep = RY // 2 * RX
    vmem = pl.BlockSpec(memory_space=pltpu.VMEM)
    anywhere = pl.BlockSpec(memory_space=pltpu.HBM)
    return pl.pallas_call(
        functools.partial(
            kernel, slab_size, orient_size, planes, float(planes * slab_size * cells)
        ),
        out_shape=pltpu.VMEM((4, width), F32),
        in_specs=[anywhere] * 7,
        out_specs=vmem,
        scratch_shapes=[
            pltpu.VMEM(pol.shape, BF16),
            pltpu.VMEM(occ.shape, jnp.int32),
            pltpu.SMEM((2, orient_table.shape[0]), jnp.int32),
            pltpu.VMEM((2, width), jnp.int32),
            pltpu.VMEM(rows.shape, BF16),
            pltpu.VMEM(columns.shape, BF16),
            pltpu.VMEM(trig.shape, BF16),
            pltpu.VMEM((planes * tiles * 2, LANES), F32),
            pltpu.VMEM((2 * group * RY, LANES), F32),
            pltpu.VMEM((max(width // LANES, 1), 2 * group, LANES), F32),
            pltpu.VMEM((2, slab_size * planes, width), F32),
            pltpu.VMEM((2, 2 * deep, width), BF16),
            pltpu.VMEM((slab_size, planes, space, 2 * deep), BF16),
            pltpu.VMEM((4, width), F32),
            pltpu.VMEM((orient_size, 4, width), F32),
            pltpu.SemaphoreType.DMA((7,)),
            pltpu.SemaphoreType.DMA((slab_size,)),
            pltpu.SemaphoreType.DMA((slab_size,)),
            pltpu.SemaphoreType.DMA((orient_size,)),
            pltpu.SemaphoreType.DMA((orient_size,)),
        ],
        compiler_params=pltpu.CompilerParams(
            collective_id=0, has_side_effects=True
        ),
    )(pol, occ, orient_table.T, dirs, rows, columns, trig)


def solution(mesh):
    return jax.shard_map(
        functools.partial(shards, mesh.shape["slab"], mesh.shape["orient"]),
        mesh=mesh,
        in_specs=(P("orient", None, None, "slab", None), P("slab", None), P(), P()),
        out_specs=P(None, "slab"),
        check_vma=False,
    )
```

time: 16.1 us -> 15.1 us (0.938)
  the two profiles are of different devices: /device:TPU:0 before, /device:TPU:1 now
where the time goes in v1:
time: 15.1 us; the launch traced here: 15 us
  Pallas kernels  14.4 us (95%)
  local copies, waits for them, and re-layouts  0.6 us (4%)
    pallas_call x1, Pallas kernels, shards(): pl.pallas_call(functools.partial(kernel, slab_size, orient_size, planes,...  14.4 us
    unnamed x1, local copies, waits for them, and re-layouts  0.6 us

profile of v1, /device:TPU:1, one launch (start us, length us, event | category | flops | bytes accessed | tf_op | source)
XLA Modules:
  0.0 15.0 jit_solution(16247816090005237179)
XLA Ops:
  0.0 14.4 %shard_map.73 = f32[4,256]{1,0:T(4,128)S(1)} custom-call(bf16[864,128]{1,0:T(8,128)(2,1)} %bitcast.12, s32[72,128]{1,0:T(8,128)} %bitcast.13, s32[2,8]{1,0:T(2,128)} %bitcast.15, s32[8,2,256]{2,1,0:T(2,128)} %bitcast.14, bf16[288,288]{1,0:T(8,128)(2,1)} %constant.6.clone.rows_hbm, bf16[192,128]{1,0:T(8,128)(2,1)} %constant.7.clone.columns_hbm, ...), custom_call_target="tpu_custom_call" | custom-call | tf_op jit(solution)/shard_map/pallas_call | solution.py:395
  14.4 0.6 %copy.10 = f32[4,256]{1,0:T(4,128)} copy(f32[4,256]{1,0:T(4,128)S(1)} %shard_map.73) | data formatting | bytes 8192

commit v2 on v1

v2 whole, which is shorter than its diff:
```python
import functools
import math

import jax
import jax.numpy as jnp
import numpy as np
from jax import lax
from jax.experimental import pallas as pl
from jax.experimental.pallas import tpu as pltpu
from jax.sharding import PartitionSpec as P

GX = 96
ORIENT_GRID = 16
THETA_GRID = 180
LANES = 128
RX = 32
RY = 24
wave_step = 0.4
MESH = pl.DeviceIdType.MESH
F32 = jnp.float32
BF16 = jnp.bfloat16
PER = LANES // math.gcd(LANES, GX)
TILES = GX // math.gcd(LANES, GX)
HALF = RX // 2
GROUPS = RY // 2 * RX // LANES


def sincos(angle):
    quarter = jnp.round(angle * (2.0 / math.pi))
    rest = angle - quarter * 1.5703125
    rest = rest - quarter * 4.83826794896619e-4
    square = rest * rest
    sine = rest + rest * square * (
        -1.6666654611e-1 + square * (8.3321608736e-3 + square * -1.9515295891e-4)
    )
    cosine = 1.0 - 0.5 * square + square * square * (
        4.166664568298827e-2
        + square * (-1.388731625493765e-3 + square * 2.443315711809948e-5)
    )
    turns = quarter.astype(jnp.int32)
    odd = (turns & 1) == 1
    sin_sign = jnp.where((turns & 2) == 2, -1.0, 1.0)
    cos_sign = jnp.where(((turns + 1) & 2) == 2, -1.0, 1.0)
    return (
        jnp.where(odd, cosine, sine) * sin_sign,
        jnp.where(odd, sine, cosine) * cos_sign,
    )


def prolate(length, count):
    band = math.cos(wave_step)
    at = np.arange(length)
    near = at[1:] * (length - at[1:]) / 2.0
    matrix = np.diag(((length - 1 - 2 * at) / 2.0) ** 2 * band) + np.diag(near, 1) + np.diag(near, -1)
    vectors = np.linalg.eigh(matrix)[1][:, ::-1][:, :count]
    middle = at - (length - 1) / 2.0
    even, odd = vectors[:, 0::2], vectors[:, 1::2]
    even = (even + even[::-1]) / 2.0
    odd = (odd - odd[::-1]) / 2.0
    even = even * np.where(even[length // 2] < 0, -1.0, 1.0)
    odd = odd * np.where(odd[length // 2] < 0, -1.0, 1.0)
    return even, odd


def split(values):
    high = np.asarray(values, np.float32).astype(jnp.bfloat16)
    low = (np.asarray(values, np.float64) - high.astype(np.float64)).astype(np.float32)
    return high, low.astype(jnp.bfloat16)


def tables(cells):
    lines = cells // GX
    tiles = cells // LANES
    even_x, odd_x = prolate(GX, RX)
    even_y, odd_y = prolate(lines, RY)
    both_y = np.stack([even_y, odd_y], axis=2).reshape(lines, RY)
    first = np.zeros((TILES, 2, RY, tiles))
    for tile in range(tiles):
        line = tile * LANES // GX
        for next_line in range(2):
            first[tile % TILES, next_line, :, tile] = both_y[line + next_line]
    first = first.reshape(TILES * 2 * RY, tiles)
    rows = np.concatenate(split(first), axis=1)
    block = np.concatenate([even_x, odd_x], axis=1)
    columns = np.concatenate(split(np.tile(block, (1, LANES // RX))), axis=0)
    pieces = []
    for even, odd in ((even_x, odd_x), (even_y, odd_y)):
        for part in (even, odd):
            length = part.shape[0]
            half = np.zeros((HALF, length // 2))
            half[: part.shape[1]] = 2.0 * part[length // 2 :].T
            pieces.append(half)
    trig = np.stack(pieces)
    high, low = split(trig)
    trig = np.concatenate([high, high, low], axis=2)
    return rows, columns, trig.reshape(4 * HALF, -1)


def high_low(values):
    high = values.astype(BF16)
    return high, (values - high.astype(F32)).astype(BF16)


def kernel(
    slab_size, orient_size, planes, cells_all,
    pol_hbm, occ_hbm, table_hbm, dirs_hbm, rows_hbm, columns_hbm, trig_hbm, out_ref,
    held_pol, held_occ, table_ref, dirs_ref, rows_ref, columns_ref, trig_ref,
    spread, halves, coef, found, turned, vv, landed, mine, parts,
    load_sem, send_sem, recv_sem, part_send, part_recv,
):
    slab = lax.axis_index("slab")
    orient = lax.axis_index("orient")
    is_odd = slab % 2 == 1
    odd = slab + 1 - slab % 2
    width = dirs_ref.shape[2]
    both = 2 * width
    all_orients = table_ref.shape[1]
    tiles = held_occ.shape[0] // planes
    pair_rows = 2 * tiles
    blocks = held_pol.shape[0] // (planes * pair_rows)
    orients = blocks // 3
    group = blocks * 2
    loads = [
        pltpu.make_async_copy(occ_hbm, held_occ, load_sem.at[0]),
        pltpu.make_async_copy(pol_hbm, held_pol, load_sem.at[1]),
        pltpu.make_async_copy(rows_hbm, rows_ref, load_sem.at[2]),
        pltpu.make_async_copy(columns_hbm, columns_ref, load_sem.at[3]),
        pltpu.make_async_copy(dirs_hbm.at[pl.ds(odd - 1, 2)], dirs_ref, load_sem.at[4]),
        pltpu.make_async_copy(table_hbm, table_ref, load_sem.at[5]),
        pltpu.make_async_copy(trig_hbm, trig_ref, load_sem.at[6]),
    ]
    for load in loads:
        load.start()

    barrier = pltpu.get_barrier_semaphore()

    def greet(plane_of, target):
        pl.semaphore_signal(
            barrier, inc=1, device_id=(plane_of, target), device_id_type=MESH
        )

    @pl.when(is_odd)
    def _():
        for step in range(1, slab_size):
            greet(orient, (slab + step) % slab_size)

    @pl.when(jnp.logical_not(is_odd))
    def _():
        greet(orient, odd)

    for step in range(1, orient_size):
        greet((orient + step) % orient_size, odd)

    for load in loads[:4]:
        load.wait()
    lane = lax.broadcasted_iota(jnp.int32, (1, LANES), 1)
    columns = [columns_ref[0:GX, :]] * PER, [columns_ref[GX : 2 * GX, :]] * PER
    columns = jnp.concatenate(columns[0] + columns[1] + columns[0], axis=0)
    for plane in range(planes):
        kept = held_occ[plane * tiles : (plane + 1) * tiles, :].astype(F32)
        for block in range(blocks):
            at = (block * planes + plane) * pair_rows
            spread[block] = held_pol[at : at + pair_rows, :].astype(F32)
            masked = jnp.concatenate(
                [spread[block, pl.ds(p, tiles, stride=2), :] * kept for p in range(2)], axis=1
            )
            lines = jnp.dot(
                rows_ref[...], jnp.concatenate([masked, masked], axis=0).astype(BF16),
                preferred_element_type=F32,
            )
            stacked = []
            for p in range(2):
                wide = []
                for j in range(TILES):
                    base = j * 2 * RY
                    at = slice(p * LANES, (p + 1) * LANES)
                    limit = GX - j * LANES % GX
                    wide.append(
                        jnp.where(
                            lane < limit,
                            lines[base : base + RY, at],
                            lines[base + RY : base + 2 * RY, at],
                        )
                    )
                stacked.append(jnp.concatenate(wide, axis=1))
            high, low = high_low(jnp.concatenate(stacked, axis=0))
            halves[0, block * 2 * RY : (block + 1) * 2 * RY, :] = high
            halves[1, block * 2 * RY : (block + 1) * 2 * RY, :] = low
        small = jnp.dot(
            jnp.concatenate([halves[0], halves[0], halves[1]], axis=1), columns,
            preferred_element_type=F32,
        )
        coef[0 : group * RY, :] = small
        coef[group * RY : 2 * group * RY, :] = small
        lines_of = [coef[pl.ds(ky, 2 * group, stride=RY), :] for ky in range(RY)]
        upper = lane % RX >= HALF
        is_low = lax.broadcasted_iota(jnp.int32, (2 * group, LANES), 0) >= group
        for imag in range(2):
            for g in range(GROUPS):
                whole = None
                for q in range(LANES // RX - 1, -1, -1):
                    a = g * (LANES // RX) + q
                    one, two = lines_of[2 * a + imag], lines_of[2 * a + 1 - imag]
                    block = jnp.where(upper, two, one)
                    whole = block if whole is None else jnp.where(lane < (q + 1) * RX, block, whole)
                high = whole.astype(BF16).astype(F32)
                at = (imag * GROUPS + g) * LANES
                landed[slab, plane, 0 : 2 * group, at : at + LANES] = jnp.where(
                    is_low, whole - high, high
                ).astype(BF16)

    pl.semaphore_wait(barrier, slab_size // 2 + slab % 2 * (2 * orient_size - 2))
    order = list(range(1, slab_size, 2))

    def slab_copy(source, target):
        piece = landed.at[source, :, pl.ds(0, 2 * group), :]
        return pltpu.make_async_remote_copy(
            src_ref=piece,
            dst_ref=piece,
            send_sem=send_sem.at[target],
            recv_sem=recv_sem.at[source],
            device_id=(orient, target),
            device_id_type=MESH,
        )

    for target in order:
        @pl.when(slab != target)
        def _():
            slab_copy(slab, target).start()

    for load in loads[4:]:
        load.wait()

    def part_copy(step, core):
        return pltpu.make_async_remote_copy(
            src_ref=mine.at[core],
            dst_ref=parts.at[orient],
            send_sem=part_send.at[core, step],
            recv_sem=part_recv.at[step],
            device_id=((orient + step) % orient_size, odd - 1 + core),
            device_id_type=MESH,
        )

    routes = [(step, core) for step in range(orient_size - 1, -1, -1) for core in range(2) if step + 1 - core]

    @pl.when(is_odd)
    def _():
        dirs = jnp.concatenate([dirs_ref[0], dirs_ref[1]], axis=1).astype(F32)
        is_polar = lax.broadcasted_iota(jnp.int32, (2, both), 0) == 0
        angles = jnp.where(
            is_polar, (dirs + 0.5) * (math.pi / THETA_GRID), dirs * (2.0 * math.pi / THETA_GRID)
        )
        sines, cosines = sincos(angles)
        sin_p, cos_p = sines[0:1], cosines[0:1]
        sin_a, cos_a = sines[1:2], cosines[1:2]
        azimuth = angles[1:2]
        normals = (sin_p * cos_a, sin_p * sin_a)
        parts_of = []
        for axis in range(2):
            length = trig_ref.shape[1] // 3
            step = lax.broadcasted_iota(jnp.int32, (length, both), 0).astype(F32) + 0.5
            sine, cosine = sincos(step * (wave_step * normals[axis]))
            for kind, wave in enumerate((cosine, sine)):
                high, low = high_low(wave)
                at = (axis * 2 + kind) * HALF
                parts_of.append(
                    jnp.dot(
                        trig_ref[at : at + HALF, :],
                        jnp.concatenate([high, low, high], axis=0),
                        preferred_element_type=F32,
                    )
                )
        even_x, odd_x, even_y, odd_y = parts_of
        deep = RY // 2 * RX
        for a in range(RY // 2):
            one, two = even_y[a : a + 1], odd_y[a : a + 1]
            for kind, pieces in enumerate(
                (
                    (even_x * one, -(odd_x * two)),
                    (even_x * two, odd_x * one),
                )
            ):
                high, low = high_low(jnp.concatenate(pieces, axis=0))
                vv[kind, a * RX : (a + 1) * RX, :] = high
                vv[kind, deep + a * RX : deep + (a + 1) * RX, :] = low

        tilt_row = lax.broadcasted_iota(jnp.int32, (all_orients, both), 0)
        tilts = jnp.zeros((all_orients, both), F32)
        for o in range(all_orients):
            tilts = jnp.where(tilt_row == o, table_ref[1, o].astype(F32), tilts)
        weights = sincos((tilts + 0.5) * (math.pi / ORIENT_GRID))[0]
        share = 1.0 / (jnp.sum(weights, axis=0, keepdims=True) * cells_all)
        own_row = lax.broadcasted_iota(jnp.int32, (2 * orients, both), 0) % orients
        turns = jnp.zeros((2 * orients, both), F32)
        tilt = jnp.zeros((2 * orients, both), F32)
        for o in range(orients):
            turns = jnp.where(own_row == o, table_ref[0, orient * orients + o].astype(F32), turns)
            tilt = jnp.where(own_row == o, table_ref[1, orient * orients + o].astype(F32), tilt)
        sin_q, cos_q = sincos(azimuth - turns * (2.0 * math.pi / ORIENT_GRID))
        weight = sincos((tilt + 0.5) * (math.pi / ORIENT_GRID))[0] * share
        depth_at = lax.broadcasted_iota(jnp.int32, (slab_size * planes, both), 0).astype(F32)
        sin_z, cos_z = sincos(depth_at * (wave_step * cos_p))
        turned[0] = cos_z
        turned[1] = sin_z

        for source in range(slab_size - 1, -1, -1):
            @pl.when(slab != source)
            def _():
                slab_copy(source, slab).wait_recv()

        space = landed.shape[2]
        everything = landed[...].reshape(slab_size * planes * space, 2 * deep)
        real_in, imag_in = everything[:, :deep], everything[:, deep:]
        real = jnp.dot(
            jnp.concatenate([real_in, real_in], axis=1), vv[0], preferred_element_type=F32
        )
        imag = jnp.dot(
            jnp.concatenate([imag_in, imag_in], axis=1), vv[1], preferred_element_type=F32
        )
        total_r = total_i = None
        for z in range(slab_size * planes):
            at = slice(z * space, z * space + 2 * group)
            c, s = turned[0, z : z + 1, :], turned[1, z : z + 1, :]
            now_r = real[at] * c - imag[at] * s
            now_i = imag[at] * c + real[at] * s
            total_r = now_r if total_r is None else total_r + now_r
            total_i = now_i if total_i is None else total_i + now_i
        total_r, total_i = total_r[:group] + total_r[group:], total_i[:group] + total_i[group:]
        piece = min(both, LANES)
        for h in range(both // piece):
            found[h, :group, :piece] = total_r[:, h * piece : (h + 1) * piece]
            found[h, group:, :piece] = total_i[:, h * piece : (h + 1) * piece]

        def entry(c, p):
            return jnp.concatenate(
                [
                    found[h, pl.ds(2 * c + p, 2 * orients, stride=6), :][:, :piece]
                    for h in range(both // piece)
                ],
                axis=1,
            )

        par, across = [], []
        for p in range(2):
            one, two, three = entry(0, p), entry(1, p), entry(2, p)
            par.append(cos_p * (one * cos_q + two * sin_q) - sin_p * three)
            across.append(two * cos_q - one * sin_q)
        par_square = par[0] * par[0] + par[1] * par[1]
        across_square = across[0] * across[0] + across[1] * across[1]

        def swap(values):
            return jnp.concatenate([values[orients:], -values[:orients]], axis=0)

        elements = (
            0.5 * (par_square + across_square),
            0.5 * (par_square - across_square),
            across[1] * par[0] + across[0] * par[1],
            par[0] * swap(across[1]) + par[1] * swap(across[0]),
        )
        result = jnp.concatenate(
            [jnp.sum(element * weight, axis=0, keepdims=True) for element in elements], axis=0
        )
        mine[0] = result[:, :width]
        mine[1] = result[:, width:]
        parts[orient] = result[:, width:]

        for step, core in routes:
            part_copy(step, core).start()

    for target in order:
        @pl.when(slab != target)
        def _():
            slab_copy(slab, target).wait_send()

    def arrival(step):
        back = (orient + orient_size - step) % orient_size
        return pltpu.make_async_remote_copy(
            src_ref=mine.at[0],
            dst_ref=parts.at[back],
            send_sem=part_send.at[0, step],
            recv_sem=part_recv.at[step],
            device_id=(back, odd),
            device_id_type=MESH,
        )

    @pl.when(jnp.logical_not(is_odd))
    def _():
        arrival(0).wait_recv()

    for step in range(1, orient_size):
        arrival(step).wait_recv()
    summed = parts[0]
    for o in range(1, orient_size):
        summed = summed + parts[o]
    out_ref[...] = summed

    @pl.when(is_odd)
    def _():
        for step, core in routes:
            part_copy(step, core).wait_send()


def shards(slab_size, orient_size, polarization, occupied, orient_table, dir_index):
    orients, _, components, planes, cells = polarization.shape
    group = orients * 6
    tiles = cells // LANES
    width = dir_index.shape[0] // slab_size
    pol = polarization.reshape(orients, 2, components, planes, tiles, LANES)
    pol = pol.transpose(0, 2, 3, 4, 1, 5).reshape(-1, LANES)
    occ = occupied.reshape(planes * tiles, LANES)
    dirs = dir_index.T.reshape(2, slab_size, width).transpose(1, 0, 2)
    rows, columns, trig = (jnp.asarray(table) for table in tables(cells))
    space = -(-2 * group // 16) * 16
    deep = RY // 2 * RX
    vmem = pl.BlockSpec(memory_space=pltpu.VMEM)
    anywhere = pl.BlockSpec(memory_space=pltpu.HBM)
    return pl.pallas_call(
        functools.partial(
            kernel, slab_size, orient_size, planes, float(planes * slab_size * cells)
        ),
        out_shape=pltpu.VMEM((4, width), F32),
        in_specs=[anywhere] * 7,
        out_specs=vmem,
        scratch_shapes=[
            pltpu.VMEM(pol.shape, BF16),
            pltpu.VMEM(occ.shape, jnp.int32),
            pltpu.SMEM((2, orient_table.shape[0]), jnp.int32),
            pltpu.VMEM((2, 2, width), jnp.int32),
            pltpu.VMEM(rows.shape, BF16),
            pltpu.VMEM(columns.shape, BF16),
            pltpu.VMEM(trig.shape, BF16),
            pltpu.VMEM((3 * orients, tiles * 2, LANES), F32),
            pltpu.VMEM((2, group * RY, TILES * LANES), BF16),
            pltpu.VMEM((2 * group * RY, LANES), F32),
            pltpu.VMEM((max(2 * width // LANES, 1), 2 * group, LANES), F32),
            pltpu.VMEM((2, slab_size * planes, 2 * width), F32),
            pltpu.VMEM((2, 2 * deep, 2 * width), BF16),
            pltpu.VMEM((slab_size, planes, space, 2 * deep), BF16),
            pltpu.VMEM((2, 4, width), F32),
            pltpu.VMEM((orient_size, 4, width), F32),
            pltpu.SemaphoreType.DMA((7,)),
            pltpu.SemaphoreType.DMA((slab_size,)),
            pltpu.SemaphoreType.DMA((slab_size,)),
            pltpu.SemaphoreType.DMA((2, orient_size)),
            pltpu.SemaphoreType.DMA((orient_size,)),
        ],
        compiler_params=pltpu.CompilerParams(
            collective_id=0, has_side_effects=True
        ),
    )(pol, occ, orient_table.T, dirs, rows, columns, trig)


def solution(mesh):
    return jax.shard_map(
        functools.partial(shards, mesh.shape["slab"], mesh.shape["orient"]),
        mesh=mesh,
        in_specs=(P("orient", None, None, "slab", None), P("slab", None), P(), P()),
        out_specs=P(None, "slab"),
        check_vma=False,
    )
```

time: 15.1 us -> 13.7 us (0.907)
  the two profiles are of different devices: /device:TPU:1 before, /device:TPU:0 now
where the time goes in v2:
time: 13.7 us; the launch traced here: 13.5 us
  Pallas kernels  12.9 us (94%)
  local copies, waits for them, and re-layouts  0.6 us (4%)
    pallas_call x1, Pallas kernels, shards(): pl.pallas_call(functools.partial(kernel, slab_size, orient_size, planes,...  12.9 us
    unnamed x1, local copies, waits for them, and re-layouts  0.6 us

profile of v2, /device:TPU:0, one launch (start us, length us, event | category | flops | bytes accessed | tf_op | source)
XLA Modules:
  0.0 13.5 jit_solution(2756798467881941169)
XLA Ops:
  0.0 12.9 %shard_map.73 = f32[4,256]{1,0:T(4,128)S(1)} custom-call(bf16[864,128]{1,0:T(8,128)(2,1)} %bitcast.12, s32[72,128]{1,0:T(8,128)} %bitcast.13, s32[2,8]{1,0:T(2,128)} %bitcast.15, s32[8,2,256]{2,1,0:T(2,128)} %bitcast.14, bf16[144,144]{1,0:T(8,128)(2,1)} %constant.6.clone.rows_hbm, bf16[192,128]{1,0:T(8,128)(2,1)} %constant.7.clone.columns_hbm, ...), custom_call_target="tpu_custom_call" | custom-call | tf_op jit(solution)/shard_map/pallas_call | solution.py:417
  12.9 0.6 %copy.10 = f32[4,256]{1,0:T(4,128)} copy(f32[4,256]{1,0:T(4,128)S(1)} %shard_map.73) | data formatting | bytes 8192

commit v3 on v2

--- a/solution.py
+++ b/solution.py
@@ -23,6 +23,7 @@
 TILES = GX // math.gcd(LANES, GX)
 HALF = RX // 2
 GROUPS = RY // 2 * RX // LANES
+LOW = 2 * LANES
 
 
 def sincos(angle):
@@ -82,7 +83,7 @@
     first = first.reshape(TILES * 2 * RY, tiles)
     rows = np.concatenate(split(first), axis=1)
     block = np.concatenate([even_x, odd_x], axis=1)
-    columns = np.concatenate(split(np.tile(block, (1, LANES // RX))), axis=0)
+    columns = np.concatenate(split(np.tile(block, (1, LANES // RX))), axis=1)
     pieces = []
     for even, odd in ((even_x, odd_x), (even_y, odd_y)):
         for part in (even, odd):
@@ -154,8 +155,7 @@
     for load in loads[:4]:
         load.wait()
     lane = lax.broadcasted_iota(jnp.int32, (1, LANES), 1)
-    columns = [columns_ref[0:GX, :]] * PER, [columns_ref[GX : 2 * GX, :]] * PER
-    columns = jnp.concatenate(columns[0] + columns[1] + columns[0], axis=0)
+    columns = jnp.concatenate([columns_ref[...]] * (2 * PER), axis=0)
     for plane in range(planes):
         kept = held_occ[plane * tiles : (plane + 1) * tiles, :].astype(F32)
         for block in range(blocks):
@@ -187,22 +187,27 @@
             halves[0, block * 2 * RY : (block + 1) * 2 * RY, :] = high
             halves[1, block * 2 * RY : (block + 1) * 2 * RY, :] = low
         small = jnp.dot(
-            jnp.concatenate([halves[0], halves[0], halves[1]], axis=1), columns,
+            jnp.concatenate([halves[0], halves[1]], axis=1), columns,
             preferred_element_type=F32,
         )
+        small = small[:, :LANES] + small[:, LANES:]
         coef[0 : group * RY, :] = small
         coef[group * RY : 2 * group * RY, :] = small
         lines_of = [coef[pl.ds(ky, 2 * group, stride=RY), :] for ky in range(RY)]
         upper = lane % RX >= HALF
         is_low = lax.broadcasted_iota(jnp.int32, (2 * group, LANES), 0) >= group
-        for imag in range(2):
-            for g in range(GROUPS):
-                whole = None
-                for q in range(LANES // RX - 1, -1, -1):
-                    a = g * (LANES // RX) + q
-                    one, two = lines_of[2 * a + imag], lines_of[2 * a + 1 - imag]
-                    block = jnp.where(upper, two, one)
-                    whole = block if whole is None else jnp.where(lane < (q + 1) * RX, block, whole)
+        share_of = LANES // RX
+        for g in range(GROUPS):
+            picked = []
+            for parity in range(2):
+                whole = lines_of[2 * (g * share_of + share_of - 1) + parity]
+                for q in range(share_of - 2, -1, -1):
+                    whole = jnp.where(
+                        lane < (q + 1) * RX, lines_of[2 * (g * share_of + q) + parity], whole
+                    )
+                picked.append(whole)
+            for imag in range(2):
+                whole = jnp.where(upper, picked[1 - imag], picked[imag])
                 high = whole.astype(BF16).astype(F32)
                 at = (imag * GROUPS + g) * LANES
                 landed[slab, plane, 0 : 2 * group, at : at + LANES] = jnp.where(
@@ -282,7 +287,8 @@
             ):
                 high, low = high_low(jnp.concatenate(pieces, axis=0))
                 vv[kind, a * RX : (a + 1) * RX, :] = high
-                vv[kind, deep + a * RX : deep + (a + 1) * RX, :] = low
+                if a * RX < LOW:
+                    vv[kind, deep + a * RX : deep + (a + 1) * RX, :] = low
 
         tilt_row = lax.broadcasted_iota(jnp.int32, (all_orients, both), 0)
         tilts = jnp.zeros((all_orients, both), F32)
@@ -311,61 +317,67 @@
         space = landed.shape[2]
         everything = landed[...].reshape(slab_size * planes * space, 2 * deep)
         real_in, imag_in = everything[:, :deep], everything[:, deep:]
-        real = jnp.dot(
-            jnp.concatenate([real_in, real_in], axis=1), vv[0], preferred_element_type=F32
-        )
-        imag = jnp.dot(
-            jnp.concatenate([imag_in, imag_in], axis=1), vv[1], preferred_element_type=F32
-        )
-        total_r = total_i = None
-        for z in range(slab_size * planes):
-            at = slice(z * space, z * space + 2 * group)
-            c, s = turned[0, z : z + 1, :], turned[1, z : z + 1, :]
-            now_r = real[at] * c - imag[at] * s
-            now_i = imag[at] * c + real[at] * s
-            total_r = now_r if total_r is None else total_r + now_r
-            total_i = now_i if total_i is None else total_i + now_i
-        total_r, total_i = total_r[:group] + total_r[group:], total_i[:group] + total_i[group:]
-        piece = min(both, LANES)
-        for h in range(both // piece):
-            found[h, :group, :piece] = total_r[:, h * piece : (h + 1) * piece]
-            found[h, group:, :piece] = total_i[:, h * piece : (h + 1) * piece]
-
-        def entry(c, p):
-            return jnp.concatenate(
-                [
-                    found[h, pl.ds(2 * c + p, 2 * orients, stride=6), :][:, :piece]
-                    for h in range(both // piece)
-                ],
-                axis=1,
+        real_in = jnp.concatenate([real_in, real_in[:, :LOW]], axis=1)
+        imag_in = jnp.concatenate([imag_in, imag_in[:, :LOW]], axis=1)
+        piece = min(width, LANES)
+        for core in range(2):
+            cut = slice(core * width, (core + 1) * width)
+            real = jnp.dot(real_in, vv[0, :, cut], preferred_element_type=F32)
+            imag = jnp.dot(imag_in, vv[1, :, cut], preferred_element_type=F32)
+            total_r = total_i = None
+            for z in range(slab_size * planes):
+                at = slice(z * space, z * space + 2 * group)
+                c, s = turned[0, z : z + 1, cut], turned[1, z : z + 1, cut]
+                now_r = real[at] * c - imag[at] * s
+                now_i = imag[at] * c + real[at] * s
+                total_r = now_r if total_r is None else total_r + now_r
+                total_i = now_i if total_i is None else total_i + now_i
+            total_r = total_r[:group] + total_r[group:]
+            total_i = total_i[:group] + total_i[group:]
+            count = width // piece
+            for h in range(count):
+                found[core * count + h, :group, :piece] = total_r[:, h * piece : (h + 1) * piece]
+                found[core * count + h, group:, :piece] = total_i[:, h * piece : (h + 1) * piece]
+
+            def entry(c, p):
+                return jnp.concatenate(
+                    [
+                        found[core * count + h, pl.ds(2 * c + p, 2 * orients, stride=6), :][:, :piece]
+                        for h in range(count)
+                    ],
+                    axis=1,
+                )
+
+            par, across = [], []
+            for p in range(2):
+                one, two, three = entry(0, p), entry(1, p), entry(2, p)
+                turned_one = one * cos_q[:, cut] + two * sin_q[:, cut]
+                par.append(cos_p[:, cut] * turned_one - sin_p[:, cut] * three)
+                across.append(two * cos_q[:, cut] - one * sin_q[:, cut])
+            par_square = par[0] * par[0] + par[1] * par[1]
+            across_square = across[0] * across[0] + across[1] * across[1]
+
+            def swap(values):
+                return jnp.concatenate([values[orients:], -values[:orients]], axis=0)
+
+            elements = (
+                0.5 * (par_square + across_square),
+                0.5 * (par_square - across_square),
+                across[1] * par[0] + across[0] * par[1],
+                par[0] * swap(across[1]) + par[1] * swap(across[0]),
             )
-
-        par, across = [], []
-        for p in range(2):
-            one, two, three = entry(0, p), entry(1, p), entry(2, p)
-            par.append(cos_p * (one * cos_q + two * sin_q) - sin_p * three)
-            across.append(two * cos_q - one * sin_q)
-        par_square = par[0] * par[0] + par[1] * par[1]
-        across_square = across[0] * across[0] + across[1] * across[1]
-
-        def swap(values):
-            return jnp.concatenate([values[orients:], -values[:orients]], axis=0)
-
-        elements = (
-            0.5 * (par_square + across_square),
-            0.5 * (par_square - across_square),
-            across[1] * par[0] + across[0] * par[1],
-            par[0] * swap(across[1]) + par[1] * swap(across[0]),
-        )
-        result = jnp.concatenate(
-            [jnp.sum(element * weight, axis=0, keepdims=True) for element in elements], axis=0
-        )
-        mine[0] = result[:, :width]
-        mine[1] = result[:, width:]
-        parts[orient] = result[:, width:]
-
-        for step, core in routes:
-            part_copy(step, core).start()
+            result = jnp.concatenate(
+                [jnp.sum(element * weight[:, cut], axis=0, keepdims=True) for element in elements],
+                axis=0,
+            )
+            if core == 0:
+                mine[0] = result
+            else:
+                mine[1] = result
+                parts[orient] = result
+            for step, target_core in routes:
+                if target_core == core:
+                    part_copy(step, core).start()
 
     for target in order:
         @pl.when(slab != target)
@@ -432,9 +444,9 @@
             pltpu.VMEM((3 * orients, tiles * 2, LANES), F32),
             pltpu.VMEM((2, group * RY, TILES * LANES), BF16),
             pltpu.VMEM((2 * group * RY, LANES), F32),
-            pltpu.VMEM((max(2 * width // LANES, 1), 2 * group, LANES), F32),
+            pltpu.VMEM((2 * max(width // LANES, 1), 2 * group, LANES), F32),
             pltpu.VMEM((2, slab_size * planes, 2 * width), F32),
-            pltpu.VMEM((2, 2 * deep, 2 * width), BF16),
+            pltpu.VMEM((2, deep + LOW, 2 * width), BF16),
             pltpu.VMEM((slab_size, planes, space, 2 * deep), BF16),
             pltpu.VMEM((2, 4, width), F32),
             pltpu.VMEM((orient_size, 4, width), F32),

time: 13.7 us -> 13.3 us (0.971)
  Pallas kernels: 12.9 us -> 12.6 us
    pallas_call x1, Pallas kernels: 12.9 us -> 12.6 us  [shards(): pl.pallas_call(functools.partial(kernel, slab_size, orient_size, planes,...]
where the time goes in v3:
time: 13.3 us; the launch traced here: 13.2 us
  Pallas kernels  12.6 us (95%)
  local copies, waits for them, and re-layouts  0.6 us (5%)
    pallas_call x1, Pallas kernels, shards(): pl.pallas_call(functools.partial(kernel, slab_size, orient_size, planes,...  12.6 us
    unnamed x1, local copies, waits for them, and re-layouts  0.6 us

profile of v3, /device:TPU:0, one launch (start us, length us, event | category | flops | bytes accessed | tf_op | source)
XLA Modules:
  0.0 13.2 jit_solution(8425776231294061160)
XLA Ops:
  0.0 12.6 %shard_map.73 = f32[4,256]{1,0:T(4,128)S(1)} custom-call(bf16[864,128]{1,0:T(8,128)(2,1)} %bitcast.12, s32[72,128]{1,0:T(8,128)} %bitcast.13, s32[2,8]{1,0:T(2,128)} %bitcast.15, s32[8,2,256]{2,1,0:T(2,128)} %bitcast.14, bf16[144,144]{1,0:T(8,128)(2,1)} %constant.6.clone.rows_hbm, bf16[96,256]{1,0:T(8,128)(2,1)} %constant.7.clone.columns_hbm, ...), custom_call_target="tpu_custom_call" | custom-call | tf_op jit(solution)/shard_map/pallas_call | solution.py:429
  12.6 0.6 %copy.10 = f32[4,256]{1,0:T(4,128)} copy(f32[4,256]{1,0:T(4,128)S(1)} %shard_map.73) | data formatting | bytes 8192
